TPU v7x, 512 devices: a whole 4x8x8 slice. The times are simulated.
512 devices in a mesh: sx: 16 (over z_lo, x, core), sy: 8 (over y), px: 4 (over z_hi).
Axes of the slice: x: 4, y: 8, z: 8 (z_hi: 4, z_lo: 2; z = z_hi * 2 + z_lo), core: 2. Of those that a mesh axis runs over, the one named last changes fastest.
Arguments:
- patterns: bfloat16 [256, 256, 9216], P('sx', 'sy', 'px'), may hold values from -6 to 6
- basis: bfloat16 [9216, 256], P('px', ('sx', 'sy')), may hold values from -0.375 to 0.375
- valid: int32 [256, 256], P('sx', 'sy'), may hold values 0 or 1
- strength: float32 [256, 256], P('sx', 'sy'), may hold values from 0.25 to 2
Outputs:
- denoised: bfloat16 [256, 256, 9216], P('sx', 'sy', 'px')
Inputs may be any that keep to these rules, and one draw needn't show every extreme that they name: `valid`: 1 marks an on-sample scan position, 0 an off-sample one.
All inputs are finite; a program needn't handle non-finite values. No bound on the sum of `valid` on one device may be relied on, other than what follows from the above.
Results may differ from a plain program's by a relative error of at most 0.0089.
Values may be sent and summed in bfloat16 or wider, within the bound.
A program may use at most 64 MiB of HBM per device.

v0:
```python
import jax
import jax.numpy as jnp
from jax import lax
from jax.sharding import Mesh
from jax.sharding import PartitionSpec as P

PIX = 9216
RADIUS = 3
SX_SY = ("sx_0", "sx_1", "sx_2", "sy")
SX = ("sx_0", "sx_1", "sx_2")


def extended(array, sides, width):
    for axis, dim in sides:
        count, length = (lax.axis_size(axis), array.shape[dim])
        up = [(i, (i + 1) % count) for i in range(count - 1)]
        down = [(j, i) for i, j in up]
        last = lax.slice_in_dim(array, length - width, length, axis=dim)
        initial = lax.slice_in_dim(array, 0, width, axis=dim)
        before = lax.ppermute(last, axis, up)
        after = lax.ppermute(initial, axis, down)
        array = jnp.concatenate([before, array, after], axis=dim)
    return array


def copy_for_each(array, axis):
    count = lax.axis_size(axis)
    return lax.all_to_all(
        jnp.broadcast_to(array[None], (count, *array.shape)), axis, 0, 0, tiled=True
    )


def joined_along(parts, dim):
    shape = list(parts.shape[1:])
    shape[dim] *= parts.shape[0]
    return jnp.moveaxis(parts, 0, dim).reshape(shape)


def gather_axes(array, axes, dim):
    far, near = axes
    parts = copy_for_each(copy_for_each(array, far), near)
    return joined_along(parts.swapaxes(0, 1).reshape(-1, *array.shape), dim)


def of_everyone(array, axis):
    return copy_for_each(array, axis).astype(jnp.float32).sum(axis=0)


def neighbour_steps():
    steps = []
    for row_step in range(-RADIUS, RADIUS + 1):
        for col_step in range(-RADIUS, RADIUS + 1):
            if row_step != 0 or col_step != 0:
                steps.append((row_step, col_step))
    return steps


def squared_gaps(center, padded):
    rows, cols = (center.shape[0], center.shape[1])
    gaps = []
    for row_step, col_step in neighbour_steps():
        other = padded[
            RADIUS + row_step : RADIUS + row_step + rows,
            RADIUS + col_step : RADIUS + col_step + cols,
        ]
        differ = center - other
        gaps.append(jnp.sum(differ * differ, axis=-1))
    return jnp.stack(gaps)


def blend(center, padded, mask_pad, gaps, strength):
    rows, cols = (center.shape[0], center.shape[1])
    factor = 1.0 / (2.0 * PIX * strength)
    numerator = center
    total = jnp.ones((rows, cols), jnp.float32)
    for index, (row_step, col_step) in enumerate(neighbour_steps()):
        other = padded[
            RADIUS + row_step : RADIUS + row_step + rows,
            RADIUS + col_step : RADIUS + col_step + cols,
        ]
        mask_other = mask_pad[
            RADIUS + row_step : RADIUS + row_step + rows,
            RADIUS + col_step : RADIUS + col_step + cols,
        ]
        weight = mask_other * jnp.exp(-gaps[index] * factor)
        numerator = numerator + weight[:, :, None] * other
        total = total + weight
    return numerator / total[:, :, None]


def extend(coeffs, mask_full):
    return (
        extended(coeffs.astype(jnp.bfloat16), ((SX, 0), ("sy", 1)), RADIUS).astype(coeffs.dtype),
        extended(mask_full.astype(jnp.bfloat16), ((SX, 0), ("sy", 1)), RADIUS).astype(
            mask_full.dtype
        ),
    )


def on_device(patterns, basis, valid, strength):
    cells_x, cells_y, pixels = patterns.shape
    flat = patterns.reshape(cells_x * cells_y, pixels)
    whole_basis = gather_axes(basis, (("sx_0", "sx_1"), ("sx_2", "sy")), 1)
    partial_value = jnp.dot(flat, whole_basis, preferred_element_type=jnp.float32)
    partial_value = partial_value.reshape(cells_x, cells_y, partial_value.shape[1])
    mask_full = valid.astype(jnp.float32)
    coeffs = of_everyone(partial_value.astype(jnp.bfloat16), "px").astype(jnp.float32)
    padded, mask_pad = extend(coeffs, mask_full)
    gaps = squared_gaps(coeffs, padded)
    average = blend(coeffs, padded, mask_pad, gaps, strength).astype(jnp.bfloat16)
    avg_flat = average.reshape(cells_x * cells_y, average.shape[2])
    rebuilt = lax.dot_general(
        avg_flat, whole_basis, (((1,), (1,)), ((), ())), preferred_element_type=jnp.float32
    )
    return rebuilt.astype(jnp.bfloat16).reshape(cells_x, cells_y, pixels)


def solution(mesh):
    finer = Mesh(
        mesh.devices.reshape(2, 4, 2, mesh.shape["sy"], mesh.shape["px"]),
        ("sx_0", "sx_1", "sx_2", "sy", "px"),
    )
    placed = (P(SX, "sy", "px"), P("px", SX_SY), P(SX, "sy"), P(SX, "sy"))
    return jax.shard_map(
        on_device, mesh=finer, in_specs=placed, out_specs=P(SX, "sy", "px"), check_vma=False
    )
```

profile of v0, /device:TPU:1, one launch (start us, length us, event | category | flops | bytes accessed | tf_op | source)
XLA Modules:
  0.0 129.9 jit_solution(5578811624357197118)
XLA Ops:
  0.0 0.9 broadcast_in_dim.6
  0.9 11.7 %all_to_all.15 = bf16[8,2304,2]{1,2,0:T(2,128)(2,1)S(1)} all-to-all(bf16[8,2304,2]{1,2,0:T(2,128)(2,1)S(1)} %broadcast_in_dim.6), channel_id=1, replica_groups=mesh['sx_0'=2,'sx_1'=4,'sx_2'=2,'sy'=8,'px'=4] {'sx_0','sx_1'}, dimensions={0} | all-to-all | bytes 147456 | tf_op jit(solution)/shard_map/all_to_all | solution.py:28
  12.6 0.6 broadcast_in_dim.7
  13.2 39.2 %all_to_all.16 = bf16[16,8,2304,2]{2,3,1,0:T(2,128)(2,1)S(1)} all-to-all(bf16[16,8,2304,2]{2,3,1,0:T(2,128)(2,1)S(1)} %broadcast_in_dim.7), channel_id=1, replica_groups=mesh['sx_0'=2,'sx_1'=4,'sx_2'=2,'sy'=8,'px'=4] {'sx_2','sy'}, dimensions={0} | all-to-all | bytes 2359296 | tf_op jit(solution)/shard_map/all_to_all | solution.py:28
  52.4 0.3 copy.11
  52.7 2.2 %copy.12 = bf16[2304,128,2]{0,2,1:T(2,128)(2,1)} copy(bf16[2304,128,2]{0,1,2:T(8,128)(2,1)S(1)} %bitcast.15) | data formatting | bytes 2359296 | tf_op jit(solution)/shard_map/transpose | solution.py:36
  54.9 2.9 %reshape.69 = bf16[2304,256]{0,1:T(8,128)(2,1)S(1)} reshape(bf16[2304,128,2]{0,2,1:T(2,128)(2,1)} %copy.12) | data formatting | bytes 2359296 | tf_op jit(solution)/shard_map/reshape | solution.py:36
  57.9 0.8 convolution_convert_fusion.1
  58.7 1.1 broadcast_in_dim.8
  59.8 9.2 %all-to-all-start.2 = ((bf16[4,16,32,256]{3,2,1,0:T(8,128)(2,1)}), bf16[4,16,32,256]{3,2,1,0:T(8,128)(2,1)}, u32[]{:S(2)}, u32[]{:S(2)}) async-start(bf16[4,16,32,256]{3,2,1,0:T(8,128)(2,1)} %broadcast_in_dim.8), calls=%async_computation.2 | async-start | bytes 2097152 | tf_op jit(solution)/shard_map/all_to_all | solution.py:28
  69.1 3.7 %collective-permute-start = (bf16[3,32]{1,0:T(4,128)(2,1)S(1)}, bf16[3,32]{1,0:T(4,128)(2,1)S(1)}, u32[]{:S(2)}, u32[]{:S(2)}) collective-permute-start(bf16[3,32]{1,0:T(4,128)(2,1)S(1)} %get-tuple-element.108), channel_id=1, source_target_pairs={{0,32},{32,64},{64,96},{96,128},{128,160},{160,192},{192,224},{224... | collective-permute-start | bytes 584 | tf_op jit(solution)/shard_map/ppermute | solution.py:20
  72.7 1.9 %collective-permute-start.1 = (bf16[3,32]{1,0:T(4,128)(2,1)S(1)}, bf16[3,32]{1,0:T(4,128)(2,1)S(1)}, u32[]{:S(2)}, u32[]{:S(2)}) collective-permute-start(bf16[3,32]{1,0:T(4,128)(2,1)S(1)} %get-tuple-element.109), channel_id=1, source_target_pairs={{32,0},{64,32},{96,64},{128,96},{160,128},{192,160},{224,192},{256... | collective-permute-start | bytes 584 | tf_op jit(solution)/shard_map/ppermute | solution.py:21
  74.7 3.4 %collective-permute-done.1 = bf16[3,32]{1,0:T(4,128)(2,1)S(1)} collective-permute-done((bf16[3,32]{1,0:T(4,128)(2,1)S(1)}, bf16[3,32]{1,0:T(4,128)(2,1)S(1)}, u32[]{:S(2)}, u32[]{:S(2)}) %collective-permute-start.1) | collective-permute-done | bytes 224 | tf_op jit(solution)/shard_map/ppermute | solution.py:21
  78.0 0.6 copy-done.3
  78.6 16.6 %all-to-all-done.2 = bf16[4,16,32,256]{3,2,1,0:T(8,128)(2,1)} async-done(((bf16[4,16,32,256]{3,2,1,0:T(8,128)(2,1)}), bf16[4,16,32,256]{3,2,1,0:T(8,128)(2,1)}, u32[]{:S(2)}, u32[]{:S(2)}) %all-to-all-start.2) | async-done | bytes 1048608 | tf_op jit(solution)/shard_map/all_to_all | solution.py:28
  95.2 1.5 %convert_reduce_fusion = f32[16,32,256]{2,1,0:T(8,128)S(1)} fusion(bf16[4,16,32,256]{3,2,1,0:T(8,128)(2,1)} %all-to-all-done.2), kind=kLoop, calls=%fused_computation.1 | loop fusion | flops 917504 | bytes 1572864 | tf_op jit(solution)/shard_map/reduce_sum | solution.py:46
  96.8 2.6 %collective-permute-start.4 = (bf16[3,32,256]{2,1,0:T(8,128)(2,1)S(1)}, bf16[3,32,256]{2,1,0:T(8,128)(2,1)S(1)}, u32[]{:S(2)}, u32[]{:S(2)}) collective-permute-start(bf16[3,32,256]{2,1,0:T(8,128)(2,1)S(1)} %get-tuple-element.104), channel_id=1, source_target_pairs={{0,32},{32,64},{64,96},{96,128},{128,160},{160,192},{192,224},{224... | collective-permute-start | bytes 147464 | tf_op jit(solution)/shard_map/ppermute | solution.py:20
  99.4 1.9 %collective-permute-start.5 = (bf16[3,32,256]{2,1,0:T(8,128)(2,1)S(1)}, bf16[3,32,256]{2,1,0:T(8,128)(2,1)S(1)}, u32[]{:S(2)}, u32[]{:S(2)}) collective-permute-start(bf16[3,32,256]{2,1,0:T(8,128)(2,1)S(1)} %get-tuple-element.105), channel_id=1, source_target_pairs={{32,0},{64,32},{96,64},{128,96},{160,128},{192,160},{224,192},{256... | collective-permute-start | bytes 147464 | tf_op jit(solution)/shard_map/ppermute | solution.py:21
  101.3 0.1 fusion.2
  101.4 5.6 %collective-permute-start.2 = (bf16[22,3]{1,0:T(8,128)(2,1)S(1)}, bf16[22,3]{1,0:T(8,128)(2,1)S(1)}, u32[]{:S(2)}, u32[]{:S(2)}) collective-permute-start(bf16[22,3]{1,0:T(8,128)(2,1)S(1)} %get-tuple-element.106), channel_id=1, source_target_pairs={{0,4},{4,8},{8,12},{12,16},{16,20},{20,24},{24,28},{1,5},{5,9},{9,... | collective-permute-start | bytes 404 | tf_op jit(solution)/shard_map/ppermute | solution.py:20
  107.0 1.3 collective-permute-start.3
  108.3 4.0 %collective-permute-start.6 = (bf16[22,3,256]{2,1,0:T(4,128)(2,1)S(1)}, bf16[22,3,256]{2,1,0:T(4,128)(2,1)S(1)}, u32[]{:S(2)}, u32[]{:S(2)}) collective-permute-start(bf16[22,3,256]{2,1,0:T(4,128)(2,1)S(1)} %get-tuple-element.102), channel_id=1, source_target_pairs={{0,4},{4,8},{8,12},{12,16},{16,20},{20,24},{24,28},{1,5},{5,9},{9,... | collective-permute-start | bytes 101384 | tf_op jit(solution)/shard_map/ppermute | solution.py:20
  112.3 1.3 collective-permute-start.7
  113.7 0.1 maximum_convert_fusion.1
  113.8 3.4 %collective-permute-done.7 = bf16[22,3,256]{2,1,0:T(4,128)(2,1)S(1)} collective-permute-done((bf16[22,3,256]{2,1,0:T(4,128)(2,1)S(1)}, bf16[22,3,256]{2,1,0:T(4,128)(2,1)S(1)}, u32[]{:S(2)}, u32[]{:S(2)}) %collective-permute-start.7) | collective-permute-done | bytes 33824 | tf_op jit(solution)/shard_map/ppermute | solution.py:21
  117.1 0.2 maximum_convert_fusion
  117.3 1.3 %multiply_reduce_fusion.45 = (f32[16,32]{1,0:T(8,128)S(1)}, f32[16,32]{1,0:T(8,128)S(1)}, f32[16,32]{1,0:T(8,128)S(1)}, f32[16,32]{1,0:T(8,128)S(1)}, f32[16,32]...) fusion(f32[16,32,256]{2,1,0:T(8,128)S(1)} %convert_reduce_fusio, ...), kind=kLoop, calls=%fused_computation.50 | loop fusion | flops 4712448 | bytes 6840320 | tf_op jit(solution)/shard_map/reduce_sum | solution.py:67
  118.6 2.0 %multiply_reduce_fusion.46 = (f32[16,32]{1,0:T(8,128)S(1)}, f32[16,32]{1,0:T(8,128)S(1)}, f32[16,32]{1,0:T(8,128)S(1)}, f32[16,32]{1,0:T(8,128)S(1)}, f32[16,32]...) fusion(f32[16,32,256]{2,1,0:T(8,128)S(1)} %convert_reduce_fusio, ...), kind=kLoop, calls=%fused_computation.51 | loop fusion | flops 7068672 | bytes 9998336 | tf_op jit(solution)/shard_map/reduce_sum | solution.py:67
  120.6 2.0 %multiply_reduce_fusion.47 = (f32[16,32]{1,0:T(8,128)S(1)}, f32[16,32]{1,0:T(8,128)S(1)}, f32[16,32]{1,0:T(8,128)S(1)}, f32[16,32]{1,0:T(8,128)S(1)}, f32[16,32]...) fusion(f32[16,32,256]{2,1,0:T(8,128)S(1)} %convert_reduce_fusio, ...), kind=kLoop, calls=%fused_computation.52 | loop fusion | flops 7068672 | bytes 9998336 | tf_op jit(solution)/shard_map/reduce_sum | solution.py:67
  122.6 0.2 add_add_fusion
  122.8 4.9 %divide_convert_fusion = bf16[16,32,256]{2,1,0:T(8,128)(2,1)S(1)} fusion(f32[16,32,256]{2,1,0:T(8,128)S(1)} %convert_reduce_fusion, f32[22,38,256]{2,1,0:T(8,128)S(1)} %maximum_convert_fusion, f32[16,32]{1,0:T(8,128)S(1)} %get-tuple-element.53, f32[16,32]{1,0:T(8,128)S(1)} %get-tuple-element.101, f32[16,32]{1,0:T(8,128)S(1)} %get-tuple-element.100, ...), kind=kLoop, calls=%fused_computation.4 | loop fusion | flops 12845056 | bytes 26052608 | tf_op jit(solution)/shard_map/convert_element_type | solution.py:110
  127.7 2.2 %convolution_convert_fusion = bf16[512,2304]{1,0:T(8,128)(2,1)} fusion(bf16[512,256]{1,0:T(8,128)(2,1)S(1)} %bitcast.16, bf16[2304,256]{0,1:T(8,128)(2,1)S(1)} %reshape.69), kind=kOutput, calls=%fused_computation | convolution fusion | flops 605159424 | bytes 3801088 | tf_op jit(solution)/shard_map/dot_general | solution.py:112
  (21 shorter events, 0.1 us)
Async XLA Ops:
  0.0 57.9 %copy-start = (bf16[16,32,2304]{2,1,0:T(8,128)(2,1)S(1)}, bf16[16,32,2304]{2,1,0:T(8,128)(2,1)}, u32[]{:S(2)}) copy-start(bf16[16,32,2304]{2,1,0:T(8,128)(2,1)} %param.4) | copy-start | bytes 7077892
  59.8 9.3 %copy-start.2 = (s32[16,32]{1,0:T(8,128)S(1)}, s32[16,32]{1,0:T(8,128)}, u32[]{:S(2)}) copy-start(s32[16,32]{1,0:T(8,128)} %param.6) | copy-start | bytes 6148
  59.8 35.4 %all-to-all-start.2 = ((bf16[4,16,32,256]{3,2,1,0:T(8,128)(2,1)}), bf16[4,16,32,256]{3,2,1,0:T(8,128)(2,1)}, u32[]{:S(2)}, u32[]{:S(2)}) async-start(bf16[4,16,32,256]{3,2,1,0:T(8,128)(2,1)} %broadcast_in_dim.8), calls=%async_computation.2 | async-start | bytes 2097152 | tf_op jit(solution)/shard_map/all_to_all | solution.py:28
  69.1 5.6 %collective-permute-start = (bf16[3,32]{1,0:T(4,128)(2,1)S(1)}, bf16[3,32]{1,0:T(4,128)(2,1)S(1)}, u32[]{:S(2)}, u32[]{:S(2)}) collective-permute-start(bf16[3,32]{1,0:T(4,128)(2,1)S(1)} %get-tuple-element.108), channel_id=1, source_target_pairs={{0,32},{32,64},{64,96},{96,128},{128,160},{160,192},{192,224},{224... | collective-permute-start | bytes 584 | tf_op jit(solution)/shard_map/ppermute | solution.py:20
  72.7 5.3 %collective-permute-start.1 = (bf16[3,32]{1,0:T(4,128)(2,1)S(1)}, bf16[3,32]{1,0:T(4,128)(2,1)S(1)}, u32[]{:S(2)}, u32[]{:S(2)}) collective-permute-start(bf16[3,32]{1,0:T(4,128)(2,1)S(1)} %get-tuple-element.109), channel_id=1, source_target_pairs={{32,0},{64,32},{96,64},{128,96},{160,128},{192,160},{224,192},{256... | collective-permute-start | bytes 584 | tf_op jit(solution)/shard_map/ppermute | solution.py:21
  78.0 0.6 copy-start.3
  95.2 18.4 %copy-start.4 = (bf16[3,32]{1,0:T(4,128)(2,1)S(1)}, bf16[3,32]{1,0:T(4,128)(2,1)}, u32[]{:S(2)}) copy-start(bf16[3,32]{1,0:T(4,128)(2,1)} %copy-done.3) | copy-start | bytes 580
  96.8 11.5 %collective-permute-start.4 = (bf16[3,32,256]{2,1,0:T(8,128)(2,1)S(1)}, bf16[3,32,256]{2,1,0:T(8,128)(2,1)S(1)}, u32[]{:S(2)}, u32[]{:S(2)}) collective-permute-start(bf16[3,32,256]{2,1,0:T(8,128)(2,1)S(1)} %get-tuple-element.104), channel_id=1, source_target_pairs={{0,32},{32,64},{64,96},{96,128},{128,160},{160,192},{192,224},{224... | collective-permute-start | bytes 147464 | tf_op jit(solution)/shard_map/ppermute | solution.py:20
  99.4 8.9 %collective-permute-start.5 = (bf16[3,32,256]{2,1,0:T(8,128)(2,1)S(1)}, bf16[3,32,256]{2,1,0:T(8,128)(2,1)S(1)}, u32[]{:S(2)}, u32[]{:S(2)}) collective-permute-start(bf16[3,32,256]{2,1,0:T(8,128)(2,1)S(1)} %get-tuple-element.105), channel_id=1, source_target_pairs={{32,0},{64,32},{96,64},{128,96},{160,128},{192,160},{224,192},{256... | collective-permute-start | bytes 147464 | tf_op jit(solution)/shard_map/ppermute | solution.py:21
  101.4 12.3 %collective-permute-start.2 = (bf16[22,3]{1,0:T(8,128)(2,1)S(1)}, bf16[22,3]{1,0:T(8,128)(2,1)S(1)}, u32[]{:S(2)}, u32[]{:S(2)}) collective-permute-start(bf16[22,3]{1,0:T(8,128)(2,1)S(1)} %get-tuple-element.106), channel_id=1, source_target_pairs={{0,4},{4,8},{8,12},{12,16},{16,20},{20,24},{24,28},{1,5},{5,9},{9,... | collective-permute-start | bytes 404 | tf_op jit(solution)/shard_map/ppermute | solution.py:20
  107.0 6.7 %collective-permute-start.3 = (bf16[22,3]{1,0:T(8,128)(2,1)S(1)}, bf16[22,3]{1,0:T(8,128)(2,1)S(1)}, u32[]{:S(2)}, u32[]{:S(2)}) collective-permute-start(bf16[22,3]{1,0:T(8,128)(2,1)S(1)} %get-tuple-element.107), channel_id=1, source_target_pairs={{4,0},{8,4},{12,8},{16,12},{20,16},{24,20},{28,24},{5,1},{9,5},{13... | collective-permute-start | bytes 404 | tf_op jit(solution)/shard_map/ppermute | solution.py:21
  108.3 5.4 %collective-permute-start.6 = (bf16[22,3,256]{2,1,0:T(4,128)(2,1)S(1)}, bf16[22,3,256]{2,1,0:T(4,128)(2,1)S(1)}, u32[]{:S(2)}, u32[]{:S(2)}) collective-permute-start(bf16[22,3,256]{2,1,0:T(4,128)(2,1)S(1)} %get-tuple-element.102), channel_id=1, source_target_pairs={{0,4},{4,8},{8,12},{12,16},{16,20},{20,24},{24,28},{1,5},{5,9},{9,... | collective-permute-start | bytes 101384 | tf_op jit(solution)/shard_map/ppermute | solution.py:20
  112.3 4.8 %collective-permute-start.7 = (bf16[22,3,256]{2,1,0:T(4,128)(2,1)S(1)}, bf16[22,3,256]{2,1,0:T(4,128)(2,1)S(1)}, u32[]{:S(2)}, u32[]{:S(2)}) collective-permute-start(bf16[22,3,256]{2,1,0:T(4,128)(2,1)S(1)} %get-tuple-element.103), channel_id=1, source_target_pairs={{4,0},{8,4},{12,8},{16,12},{20,16},{24,20},{28,24},{5,1},{9,5},{13... | collective-permute-start | bytes 101384 | tf_op jit(solution)/shard_map/ppermute | solution.py:21
  120.6 2.0 %copy-start.1 = (f32[16,32]{1,0:T(8,128)S(1)}, f32[16,32]{1,0:T(8,128)}, u32[]{:S(2)}) copy-start(f32[16,32]{1,0:T(8,128)} %param.7) | copy-start | bytes 6148
where the time goes:
time: 132 us; the launch traced here: 130 us
  blocking collectives  50.9 us (39%)
  starting transfers between devices  31.5 us (24%)
  waiting for transfers between devices  23.3 us (18%)
  other arithmetic  12.1 us (9%)
  local copies, waits for them, and re-layouts  8.78 us (7%)
  matrix products  3.01 us (2%)
    all_to_all x2, blocking collectives, copy_for_each(): lax.all_to_all(jnp.broadcast_to(array[None], (count, *array.shape)), axis...  50.9 us
    all_to_all x1, waiting for transfers between devices, copy_for_each(): lax.all_to_all(jnp.broadcast_to(array[None], (count, *array.shape)), axis...  16.6 us
    ppermute x4, starting transfers between devices, extended(): before = lax.ppermute(last, axis, up)  15.9 us
    all_to_all x1, starting transfers between devices, copy_for_each(): lax.all_to_all(jnp.broadcast_to(array[None], (count, *array.shape)), axis...  9.25 us
    ppermute x4, waiting for transfers between devices, extended(): after = lax.ppermute(initial, axis, down)  6.73 us
    ppermute x4, starting transfers between devices, extended(): after = lax.ppermute(initial, axis, down)  6.43 us
    reduce_sum x3, other arithmetic, squared_gaps(): gaps.append(jnp.sum(differ * differ, axis=-1))  5.26 us
    convert_element_type x1, other arithmetic, on_device(): blend(coeffs, padded, mask_pad, gaps, strength).astype(jnp.bfloat16)  4.86 us
  transfers between devices with their start and end apart: 9, of which 3 were waited for; matrix products, arithmetic and copies ran while one was open for 0% of the time, Pallas kernels for 0%

commit v1 on v0

v1 whole, which is shorter than its diff:
```python
import functools
import math

import jax
import jax.numpy as jnp
from jax import lax
from jax.experimental import pallas as pl
from jax.experimental.pallas import tpu as pltpu
from jax.sharding import PartitionSpec as P

MESH = pl.DeviceIdType.MESH
RADIUS = 3
NEAR = (2, 4, 2)
FAR = 1e15
OFF = 1e30
EDGE = 4
ROWS = 4


def kernel(
    near, pix_total, patterns_ref, basis_ref, valid_ref, strength_ref,
    avg_ref, gath_ref,
    pat, pieces, stage, own32, part16, arrived, coeff, ext, halo, pack, pick, bias,
    pat_sem, send_sem, recv_sem,
):
    n_z, n_x, n_core = near
    n_sy, n_px = lax.axis_size("sy"), lax.axis_size("px")
    n_sx = n_z * n_x * n_core
    sx, sy, px = lax.axis_index("sx"), lax.axis_index("sy"), lax.axis_index("px")
    core = sx % n_core
    chip_x = (sx // n_core) % n_x
    chip_z = sx // (n_core * n_x)
    depth = basis_ref.shape[0]
    part, rank = part16.shape[1], part16.shape[2]
    cols = part // ROWS

    def at(dz, dx):
        return (((chip_z + dz + n_z) % n_z) * n_x + (chip_x + dx + n_x) % n_x) * n_core + core

    sibling = sx + 1 - 2 * core
    up, down = (sx + 1) % n_sx, (sx + n_sx - 1) % n_sx
    right, left = (sy + 1) % n_sy, (sy + n_sy - 1) % n_sy
    plane = [(dz, dx) for dx in range(n_x) for dz in range(n_z) if (dz, dx) != (0, 0)]

    load = pltpu.make_async_copy(patterns_ref, pat, pat_sem)
    load.start()

    partners = [{"sy": (sy + d) % n_sy} for d in range(1, n_sy)]
    partners += [{"sx": at(dz, dx)} for dz, dx in plane]
    partners += [{"px": (px + d) % n_px} for d in range(1, n_px)]
    partners += [{"sx": sibling}, {"sx": up}, {"sx": down}]
    partners += [{"sx": a, "sy": b} for a in (up, down) for b in (left, right)]

    def device(partner):
        return {"sx": sx, "sy": sy, "px": px, **partner}

    barrier = pltpu.get_barrier_semaphore()
    for partner in partners:
        pl.semaphore_signal(barrier, inc=1, device_id=device(partner), device_id_type=MESH)

    row = lax.broadcasted_iota(jnp.int32, pick.shape, 0)
    col = lax.broadcasted_iota(jnp.int32, pick.shape, 1)
    half = pick.shape[0] // 2
    side = row // half
    wanted = ((row % half) // EDGE) * cols + row % EDGE + side * (cols - EDGE)
    pick[...] = jnp.where(col == wanted, 1.0, 0.0).astype(pick.dtype)

    mine = lax.broadcasted_iota(jnp.int32, bias.shape, 0)
    other = lax.broadcasted_iota(jnp.int32, bias.shape, 1)
    n_mid = (ROWS + 2 * RADIUS) * cols
    n_edge = 3 * 2 * ROWS * EDGE
    edge = other - n_mid
    spot = edge % (ROWS * EDGE)
    side = (edge // (ROWS * EDGE)) % 2
    in_mid = other < n_mid
    other_row = jnp.where(in_mid, other // cols - RADIUS, (edge // (2 * ROWS * EDGE)) * ROWS + spot // EDGE - ROWS)
    other_col = jnp.where(in_mid, other % cols, spot % EDGE + jnp.where(side == 0, cols, -EDGE))
    d_row, d_col = other_row - mine // cols, other_col - mine % cols
    inside = (jnp.abs(d_row) <= RADIUS) & (jnp.abs(d_col) <= RADIUS) & (other < n_mid + n_edge)
    inside = inside & ((d_row != 0) | (d_col != 0))
    bias[...] = jnp.where(inside, 0.0, OFF)

    pl.semaphore_wait(barrier, len(partners))

    sent = []

    def send(src, dst, partner):
        k = len(sent)
        copy = pltpu.make_async_remote_copy(
            src_ref=src, dst_ref=dst, send_sem=send_sem.at[k], recv_sem=recv_sem.at[k],
            device_id=device(partner), device_id_type=MESH,
        )
        copy.start()
        sent.append(copy)
        return copy

    order = sorted(range(1, n_sy), key=lambda d: -min(d, n_sy - d))
    along = [send(basis_ref, pieces.at[sy], {"sy": (sy + d) % n_sy}) for d in order]
    pieces[pl.ds(sy, 1)] = basis_ref[...][None]
    for copy in along:
        copy.wait_recv()
    for y in range(n_sy):
        stage[depth * y:depth * (y + 1), :] = pieces[y].astype(jnp.float32)
    gath_ref[sx] = stage[...].astype(gath_ref.dtype)

    across = [(dz, dx, send(gath_ref.at[sx], gath_ref.at[sx], {"sx": at(dz, dx)})) for dz, dx in plane]
    passed = [send(gath_ref.at[sx], gath_ref.at[sx], {"sx": sibling})]
    for dz, dx, copy in across:
        copy.wait_recv()
        tile = at(-dz, -dx)
        passed.append(send(gath_ref.at[tile], gath_ref.at[tile], {"sx": sibling}))
    load.wait()
    for copy in passed:
        copy.wait_recv()

    whole = gath_ref[...].reshape(rank, gath_ref.shape[2])

    def project(which):
        block = pat[pl.ds(pl.multiple_of(which * part, part), part), :]
        return lax.dot_general(block, whole, (((1,), (1,)), ((), ())), preferred_element_type=jnp.float32)

    reduce = []
    far_first = sorted(range(1, n_px), key=lambda d: -min(d, n_px - d))
    for d in far_first:
        part16[d] = project((px + d) % n_px).astype(part16.dtype)
        reduce.append(send(part16.at[d], arrived.at[d], {"px": (px + d) % n_px}))
    own32[...] = project(px)
    for copy in reduce:
        copy.wait_recv()
    total = own32[...]
    for d in range(1, n_px):
        total = total + arrived[d].astype(jnp.float32)
    coeff[px] = total.astype(coeff.dtype)
    spread = [send(coeff.at[px], coeff.at[px], {"px": (px + d) % n_px}) for d in far_first]
    for copy in spread:
        copy.wait_recv()

    valid = jnp.transpose(valid_ref[...].astype(jnp.float32))
    n_rows = n_px * ROWS
    for r in range(n_rows):
        values = coeff[r // ROWS, (r % ROWS) * cols:(r % ROWS + 1) * cols, :].astype(jnp.float32)
        ext[RADIUS + r] = jnp.where(valid[:, r:r + 1] > 0.5, values, FAR).astype(ext.dtype)
    tile = ext[RADIUS:RADIUS + n_rows].reshape(n_rows * cols, rank)
    edges = jnp.dot(pick[...], tile, preferred_element_type=jnp.float32).astype(pack.dtype)
    pack[...] = edges.reshape(pack.shape)
    last = n_px - 1
    swap = [
        send(pack.at[0, 0], halo.at[n_px + 1, 0], {"sx": down, "sy": left}),
        send(pack.at[0, last], halo.at[0, 0], {"sx": up, "sy": left}),
        send(pack.at[1, 0], halo.at[n_px + 1, 1], {"sx": down, "sy": right}),
        send(pack.at[1, last], halo.at[0, 1], {"sx": up, "sy": right}),
        send(ext.at[pl.ds(RADIUS, RADIUS)], ext.at[pl.ds(RADIUS + n_rows, RADIUS)], {"sx": down}),
        send(ext.at[pl.ds(n_rows, RADIUS)], ext.at[pl.ds(0, RADIUS)], {"sx": up}),
        send(pack.at[0], halo.at[pl.ds(1, n_px), 0], {"sy": left}),
        send(pack.at[1], halo.at[pl.ds(1, n_px), 1], {"sy": right}),
    ]
    for copy in swap:
        copy.wait_recv()

    @pl.when(sx == 0)
    def _():
        ext[0:RADIUS] = jnp.full((RADIUS, cols, rank), FAR, ext.dtype)
        halo[0] = jnp.full(halo.shape[1:], FAR, halo.dtype)

    @pl.when(sx == n_sx - 1)
    def _():
        ext[RADIUS + n_rows:] = jnp.full((RADIUS, cols, rank), FAR, ext.dtype)
        halo[n_px + 1] = jnp.full(halo.shape[1:], FAR, halo.dtype)

    @pl.when(sy == 0)
    def _():
        halo[:, 1] = jnp.full((n_px + 2,) + halo.shape[2:], FAR, halo.dtype)

    @pl.when(sy == n_sy - 1)
    def _():
        halo[:, 0] = jnp.full((n_px + 2,) + halo.shape[2:], FAR, halo.dtype)

    factor = (math.log2(math.e) / (2.0 * pix_total)) / jnp.transpose(strength_ref[...])
    n_pad = bias.shape[1] - n_mid - n_edge
    for b in range(n_px):
        center = coeff[b]
        center32 = center.astype(jnp.float32)
        around = jnp.concatenate(
            [
                ext[ROWS * b:ROWS * b + ROWS + 2 * RADIUS].reshape(n_mid, rank),
                halo[b:b + 3].reshape(n_edge, rank),
                jnp.zeros((n_pad, rank), ext.dtype),
            ],
            axis=0,
        )
        around32 = around.astype(jnp.float32)
        inner = lax.dot_general(center, around, (((1,), (1,)), ((), ())), preferred_element_type=jnp.float32)
        size_other = lax.dot_general(
            jnp.ones((8, rank), jnp.float32), around32 * around32, (((1,), (1,)), ((), ())),
            precision=lax.Precision.HIGHEST, preferred_element_type=jnp.float32,
        )[0:1]
        size_mine = jnp.sum(center32 * center32, axis=1, keepdims=True)
        scale = jnp.concatenate([factor[:, ROWS * b + r:ROWS * b + r + 1] for r in range(ROWS)], axis=0)
        gap = jnp.maximum(size_mine + size_other - 2.0 * inner, 0.0)
        weight = jnp.exp2(-(gap * scale + bias[...])).astype(jnp.bfloat16)
        summed = jnp.dot(weight, around, preferred_element_type=jnp.float32)
        mass = jnp.sum(weight.astype(jnp.float32), axis=1, keepdims=True)
        avg_ref[b] = ((center32 + summed) / (1.0 + mass)).astype(avg_ref.dtype)

    for copy in sent:
        copy.wait_send()


def on_device(near, pix_total, patterns, basis, valid, strength):
    cells_x, cells_y, pixels = patterns.shape
    n_sx, n_sy, n_px = (lax.axis_size(name) for name in ("sx", "sy", "px"))
    depth = basis.shape[1]
    rank = depth * n_sx * n_sy
    part = cells_x * cells_y // n_px
    bf16, f32 = jnp.bfloat16, jnp.float32
    n_copies = (n_sy - 1) + 2 * (n_sx // 2 - 1) + 1 + 2 * (n_px - 1) + 8
    n_around = (ROWS + 2 * RADIUS) * cells_y + 6 * ROWS * EDGE
    n_around = -(-n_around // 128) * 128
    vmem = pl.BlockSpec(memory_space=pltpu.VMEM)
    avg, gathered = pl.pallas_call(
        functools.partial(kernel, near, pix_total),
        out_shape=(
            jax.ShapeDtypeStruct((n_px, part, rank), bf16),
            jax.ShapeDtypeStruct((n_sx, depth * n_sy, pixels), bf16),
        ),
        in_specs=[pl.BlockSpec(memory_space=pl.ANY), vmem, vmem, vmem],
        out_specs=(vmem, vmem),
        scratch_shapes=[
            pltpu.VMEM((n_px * part, pixels), bf16),
            pltpu.VMEM((n_sy, depth, pixels), bf16),
            pltpu.VMEM((n_sy * depth, pixels), f32),
            pltpu.VMEM((part, rank), f32),
            pltpu.VMEM((n_px, part, rank), bf16),
            pltpu.VMEM((n_px, part, rank), bf16),
            pltpu.VMEM((n_px, part, rank), bf16),
            pltpu.VMEM((cells_x + 2 * RADIUS, cells_y, rank), bf16),
            pltpu.VMEM((n_px + 2, 2, ROWS * EDGE, rank), bf16),
            pltpu.VMEM((2, n_px, ROWS * EDGE, rank), bf16),
            pltpu.VMEM((2 * cells_x * EDGE, cells_x * cells_y), bf16),
            pltpu.VMEM((part, n_around), f32),
            pltpu.SemaphoreType.DMA,
            pltpu.SemaphoreType.DMA((n_copies,)),
            pltpu.SemaphoreType.DMA((n_copies,)),
        ],
        compiler_params=pltpu.CompilerParams(collective_id=0, has_side_effects=True),
    )(patterns.reshape(cells_x * cells_y, pixels), basis.T, valid, strength)
    rebuilt = jnp.dot(
        avg.reshape(cells_x * cells_y, rank), gathered.reshape(rank, pixels), preferred_element_type=f32
    )
    return rebuilt.astype(bf16).reshape(cells_x, cells_y, pixels)


def solution(mesh, near=NEAR, pix_total=9216):
    return jax.shard_map(
        functools.partial(on_device, near, pix_total),
        mesh=mesh,
        in_specs=(P("sx", "sy", "px"), P("px", ("sx", "sy")), P("sx", "sy"), P("sx", "sy")),
        out_specs=P("sx", "sy", "px"),
        check_vma=False,
    )
```

time: 132 us -> 59 us (0.45); the launches traced: 130 us -> 58.8 us
  Pallas kernels: 0 us -> 55.2 us
  blocking collectives: 50.9 us -> 0 us
  starting transfers between devices: 31.5 us -> 0 us
  waiting for transfers between devices: 23.3 us -> 0 us
  other arithmetic: 12.1 us -> 0 us
  local copies, waits for them, and re-layouts: 8.78 us -> 0 us
    pallas_call x0 -> x1, Pallas kernels: none -> 55.2 us  [on_device(): pl.pallas_call(functools.partial(kernel, near, pix_total), out_shape=(jax...]
    all_to_all x2 -> x0, blocking collectives: 50.9 us -> none  [copy_for_each(): lax.all_to_all(jnp.broadcast_to(array[None], (count, *array.shape)), axis...]
    ppermute x8 -> x0, starting transfers between devices: 22.3 us -> none  [the longest x4 15.9 us: extended(): before = lax.ppermute(last, axis, up)]
    all_to_all x1 -> x0, waiting for transfers between devices: 16.6 us -> none  [copy_for_each(): lax.all_to_all(jnp.broadcast_to(array[None], (count, *array.shape)), axis...]
    all_to_all x1 -> x0, starting transfers between devices: 9.25 us -> none  [copy_for_each(): lax.all_to_all(jnp.broadcast_to(array[None], (count, *array.shape)), axis...]
    ppermute x8 -> x0, waiting for transfers between devices: 6.74 us -> none  [the longest x4 6.73 us: extended(): after = lax.ppermute(initial, axis, down)]
    reduce_sum x4 -> x0, other arithmetic: 6.74 us -> none  [the longest x3 5.26 us: squared_gaps(): gaps.append(jnp.sum(differ * differ, axis=-1))]
    convert_element_type x5 -> x0, other arithmetic: 5.14 us -> none  [the longest x1 4.86 us: on_device(): blend(coeffs, padded, mask_pad, gaps, strength).astype(jnp.bfloat16)]
  transfers between devices with their start and end apart: 9 -> 0, of which waited for: 3 -> 0; matrix products, arithmetic and copies ran while one was open for 0% -> 0% of each run, Pallas kernels for 0% -> 0%
where the time goes in v1:
time: 59 us; the launch traced here: 58.8 us
  Pallas kernels  55.2 us (94%)
  matrix products  3.55 us (6%)
    pallas_call x1, Pallas kernels, on_device(): pl.pallas_call(functools.partial(kernel, near, pix_total), out_shape=(jax...  55.2 us
    dot_general x1, matrix products, on_device(): jnp.dot(avg.reshape(cells_x * cells_y, rank), gathered.reshape(rank, pixe...  3.55 us

profile of v1, /device:TPU:1, one launch (start us, length us, event | category | flops | bytes accessed | tf_op | source)
XLA Modules:
  0.0 58.8 jit_solution(16324637535601337985)
XLA Ops:
  0.0 55.2 %shard_map.46 = (bf16[4,128,256]{2,1,0:T(8,128)(2,1)}, bf16[16,16,2304]{2,1,0:T(8,128)(2,1)}) custom-call(bf16[512,2304]{1,0:T(8,128)(2,1)} %bitcast.7, bf16[2,2304]{1,0:T(2,128)(2,1)} %bitcast.10, s32[16,32]{1,0:T(8,128)} %valid_ref.1, f32[16,32]{1,0:T(8,128)} %strength_ref.1), custom_call_target="tpu_custom_call" | custom-call | tf_op jit(solution)/shard_map/pallas_call | solution.py:220
  55.2 3.5 %convolution_convert_fusion = bf16[512,2304]{1,0:T(8,128)(2,1)} fusion(bf16[512,256]{1,0:T(8,128)(2,1)} %bitcast.9, bf16[256,2304]{1,0:T(8,128)(2,1)} %bitcast.8), kind=kOutput, calls=%fused_computation | convolution fusion | flops 605159424 | bytes 3801088 | tf_op jit(solution)/shard_map/dot_general | solution.py:247

commit v2 on v1

v2 whole, which is shorter than its diff:
```python
import functools
import math

import jax
import jax.numpy as jnp
from jax import lax
from jax.experimental import pallas as pl
from jax.experimental.pallas import tpu as pltpu
from jax.sharding import PartitionSpec as P

MESH = pl.DeviceIdType.MESH
RADIUS = 3
NEAR = (2, 4, 2)
FAR = 1e15
OFF = 1e30
EDGE = 4
ROWS = 4
NT = (((1,), (1,)), ((), ()))


def across(column):
    n = column.shape[0]
    eye = lax.broadcasted_iota(jnp.int32, (n, n), 0) == lax.broadcasted_iota(jnp.int32, (n, n), 1)
    return jnp.sum(jnp.where(eye, column, 0.0), axis=0, keepdims=True)


def norms(values):
    wide = values.astype(jnp.float32)
    return jnp.sum(wide * wide, axis=1, keepdims=True)


def outside(d_row, d_col, known):
    near = (jnp.abs(d_row) <= RADIUS) & (jnp.abs(d_col) <= RADIUS) & known
    return jnp.where(near & ((d_row != 0) | (d_col != 0)), 0.0, OFF)


def weigh(center, size, scale, around, sizes, bias):
    inner = lax.dot_general(center, around, NT, preferred_element_type=jnp.float32)
    gap = jnp.maximum(size + sizes - 2.0 * inner, 0.0)
    weight = jnp.exp2(-(gap * scale + bias)).astype(jnp.bfloat16)
    summed = jnp.dot(weight, around, preferred_element_type=jnp.float32)
    return summed, jnp.sum(weight.astype(jnp.float32), axis=1, keepdims=True)


def kernel(
    near, pix_total, patterns_ref, basis_ref, valid_ref, strength_ref,
    avg_ref, gath_ref,
    pat, pieces, own32, part16, arrived, coeff, seen, rim, halo, pack, pick, bias, bias_top, bias_low, bias_side,
    size_col, size_row, around_num, around_mass, valid_v, strength_v,
    pat_sem, basis_sem, map_sem, send_sem, recv_sem,
):
    n_z, n_x, n_core = near
    n_sy, n_px = lax.axis_size("sy"), lax.axis_size("px")
    n_sx = n_z * n_x * n_core
    sx, sy, px = lax.axis_index("sx"), lax.axis_index("sy"), lax.axis_index("px")
    core = sx % n_core
    chip_x = (sx // n_core) % n_x
    chip_z = sx // (n_core * n_x)
    depth, pixels = pieces.shape[2], pieces.shape[3]
    part, rank = own32.shape
    cols = part // ROWS
    n_rows = n_px * ROWS
    pad = RADIUS * cols
    f32, bf16 = jnp.float32, jnp.bfloat16

    def at(dz, dx):
        return (((chip_z + dz + n_z) % n_z) * n_x + (chip_x + dx + n_x) % n_x) * n_core + core

    sibling = sx + 1 - 2 * core
    up, down = (sx + 1) % n_sx, (sx + n_sx - 1) % n_sx
    right, left = (sy + 1) % n_sy, (sy + n_sy - 1) % n_sy
    hops = [min(d, n_x - d) for d in range(n_x)]
    plane = sorted(((dz, dx) for dx in range(n_x) for dz in range(n_z) if (dz, dx) != (0, 0)), key=lambda c: c[0] + hops[c[1]])

    load_basis = pltpu.make_async_copy(basis_ref, pieces.at[sx, sy], basis_sem)
    load_basis.start()
    load_maps = [
        pltpu.make_async_copy(valid_ref, valid_v, map_sem.at[0]),
        pltpu.make_async_copy(strength_ref, strength_v, map_sem.at[1]),
    ]
    for copy in load_maps:
        copy.start()
    load = pltpu.make_async_copy(patterns_ref, pat, pat_sem)
    load.start()

    partners = [{"sy": (sy + d) % n_sy} for d in range(1, n_sy)]
    partners += [{"sx": at(dz, dx)} for dz, dx in plane]
    partners += [{"px": (px + d) % n_px} for d in range(1, n_px)]
    partners += [{"sx": sibling}, {"sx": up}, {"sx": down}]
    partners += [{"sx": a, "sy": b} for a in (up, down) for b in (left, right)]

    def device(partner):
        return {"sx": sx, "sy": sy, "px": px, **partner}

    barrier = pltpu.get_barrier_semaphore()
    for partner in partners:
        pl.semaphore_signal(barrier, inc=1, device_id=device(partner), device_id_type=MESH)

    row = lax.broadcasted_iota(jnp.int32, pick.shape, 0)
    col = lax.broadcasted_iota(jnp.int32, pick.shape, 1)
    side, spot = row // (ROWS * EDGE), row % (ROWS * EDGE)
    pick[...] = jnp.where(col == (spot // EDGE) * cols + spot % EDGE + side * (cols - EDGE), 1.0, 0.0).astype(bf16)

    mine = lax.broadcasted_iota(jnp.int32, (part, 128), 0)
    lane = lax.broadcasted_iota(jnp.int32, (part, 128), 1)
    my_row, my_col = mine // cols, mine % cols
    n_mid = (ROWS + 2 * RADIUS) * cols
    n_side = 3 * 2 * ROWS * EDGE
    for k in range(bias.shape[1] // 128):
        spot = lane + 128 * k
        bias[:, 128 * k:128 * (k + 1)] = outside(spot // cols - RADIUS - my_row, spot % cols - my_col, spot < n_mid)
    spot = lane % (ROWS * EDGE)
    side_row = (lane // (2 * ROWS * EDGE)) * ROWS + spot // EDGE - ROWS
    side_col = spot % EDGE + jnp.where((lane // (ROWS * EDGE)) % 2 == 0, cols, -EDGE)
    bias_side[...] = outside(side_row - my_row, side_col - my_col, lane < n_side)
    bias_top[...] = outside(lane // cols - RADIUS - my_row, lane % cols - my_col, lane < pad)
    bias_low[...] = outside(lane // cols + ROWS - my_row, lane % cols - my_col, lane < pad)
    coeff[0:pad] = jnp.zeros((pad, rank), bf16)
    coeff[pad + n_px * part:] = jnp.zeros((coeff.shape[0] - pad - n_px * part, rank), bf16)
    size_row[...] = jnp.full(size_row.shape, OFF, f32)

    load_basis.wait()
    pl.semaphore_wait(barrier, len(partners))

    sent = []
    n_send = [0]

    def remote(src, dst, partner, k):
        return pltpu.make_async_remote_copy(
            src_ref=src, dst_ref=dst, send_sem=send_sem.at[k], recv_sem=recv_sem.at[k],
            device_id=device(partner), device_id_type=MESH,
        )

    def fresh():
        n_send[0] += 1
        return n_send[0] - 1

    def send(src, dst, partner):
        copy = remote(src, dst, partner, fresh())
        copy.start()
        sent.append(copy)
        return copy

    order = sorted(range(1, n_sy), key=lambda d: -min(d, n_sy - d))
    along = {d: send(pieces.at[sx, sy], pieces.at[sx, sy], {"sy": (sy + d) % n_sy}) for d in order}
    plane_sem = {c: fresh() for c in plane}

    def to_plane(y):
        for dz, dx in plane:
            remote(pieces.at[sx, y], pieces.at[sx, y], {"sx": at(dz, dx)}, plane_sem[dz, dx]).start()

    to_plane(sy)
    for d in reversed(order):
        along[d].wait_recv()
        to_plane((sy + n_sy - d) % n_sy)

    passed = [(sx, send(pieces.at[sx], pieces.at[sx], {"sx": sibling}))]
    merge_tile(pieces, gath_ref, sx)
    for dz, dx in plane:
        tile = at(-dz, -dx)
        remote(pieces.at[tile], pieces.at[tile], {"sx": at(dz, dx)}, plane_sem[dz, dx]).wait_recv()
        passed.append((tile, send(pieces.at[tile], pieces.at[tile], {"sx": sibling})))
        merge_tile(pieces, gath_ref, tile)
    for tile, copy in passed:
        copy.wait_recv()
        merge_tile(pieces, gath_ref, tile + 1 - 2 * core)
    load.wait()

    whole = gath_ref[...].reshape(rank, pixels)

    def project(which):
        block = pat[pl.ds(pl.multiple_of(which * part, part), part), :]
        return lax.dot_general(block, whole, NT, preferred_element_type=f32)

    reduce = []
    far_first = sorted(range(1, n_px), key=lambda d: -min(d, n_px - d))
    for d in far_first:
        part16[d] = project((px + d) % n_px).astype(bf16)
        reduce.append(send(part16.at[d], arrived.at[d], {"px": (px + d) % n_px}))
    own32[...] = project(px)
    for copy in load_maps:
        copy.wait()
    valid = jnp.transpose(valid_v[...].astype(f32))
    factor = (math.log2(math.e) / (2.0 * pix_total)) / jnp.transpose(strength_v[...])
    for b in range(n_px):
        for r in range(ROWS):
            size_col[b, cols * r:cols * (r + 1), 0:1] = valid[:, ROWS * b + r:ROWS * b + r + 1]
            size_col[b, cols * r:cols * (r + 1), 1:2] = factor[:, ROWS * b + r:ROWS * b + r + 1]
    for copy in reduce:
        copy.wait_recv()
    total = own32[...]
    for d in range(1, n_px):
        total = total + arrived[d].astype(f32)

    def slot(which):
        return coeff.at[pl.ds(pl.multiple_of(pad + which * part, ROWS * EDGE), part)]

    slot(px)[...] = total.astype(bf16)
    spread = [(d, send(slot(px), slot(px), {"px": (px + d) % n_px})) for d in far_first]

    def look(which):
        values = slot(which)[...]
        on = size_col[which, :, 0:1] > 0.5
        size = norms(values)
        size_col[which, :, 2:3] = size
        shown = jnp.where(on, values.astype(f32), FAR).astype(bf16)
        seen[which] = shown
        edges = jnp.dot(pick[...], shown, preferred_element_type=f32).astype(bf16)
        pack[0, which] = edges[:ROWS * EDGE]
        pack[1, which] = edges[ROWS * EDGE:]

    look(px)
    for d, copy in reversed(spread):
        copy.wait_recv()
        look((px + n_px - d) % n_px)
    last = n_px - 1
    swap = [
        send(seen.at[0, pl.ds(0, pad)], rim.at[1], {"sx": down}),
        send(seen.at[last, pl.ds(part - pad, pad)], rim.at[0], {"sx": up}),
        send(pack.at[0, 0], halo.at[n_px + 1, 0], {"sx": down, "sy": left}),
        send(pack.at[0, last], halo.at[0, 0], {"sx": up, "sy": left}),
        send(pack.at[1, 0], halo.at[n_px + 1, 1], {"sx": down, "sy": right}),
        send(pack.at[1, last], halo.at[0, 1], {"sx": up, "sy": right}),
        send(pack.at[0], halo.at[pl.ds(1, n_px), 0], {"sy": left}),
        send(pack.at[1], halo.at[pl.ds(1, n_px), 1], {"sy": right}),
    ]

    for b in range(n_px):
        column = jnp.where(size_col[b, :, 0:1] > 0.5, size_col[b, :, 2:3], OFF)
        size_row[0:1, 128 * b + 128:128 * b + 128 + part] = across(column)
    n_wide = bias.shape[1]
    for b in range(n_px):
        center = coeff[pad + part * b:pad + part * (b + 1)]
        lanes = 128 - pad + part * b
        sizes = jnp.concatenate([size_row[0:1, lanes:lanes + n_wide]], axis=1)
        around_num[b], around_mass[b] = weigh(
            center, size_col[b, :, 2:3], size_col[b, :, 1:2], coeff[part * b:part * b + n_wide], sizes, bias[...]
        )

    for copy in swap:
        copy.wait_recv()

    @pl.when(sx == 0)
    def _():
        rim[0] = jnp.full(rim.shape[1:], FAR, bf16)
        halo[0] = jnp.full(halo.shape[1:], FAR, bf16)

    @pl.when(sx == n_sx - 1)
    def _():
        rim[1] = jnp.full(rim.shape[1:], FAR, bf16)
        halo[n_px + 1] = jnp.full(halo.shape[1:], FAR, bf16)

    @pl.when(sy == 0)
    def _():
        halo[:, 1] = jnp.full((n_px + 2,) + halo.shape[2:], FAR, bf16)

    @pl.when(sy == n_sy - 1)
    def _():
        halo[:, 0] = jnp.full((n_px + 2,) + halo.shape[2:], FAR, bf16)

    def filled(values):
        return jnp.concatenate([values, jnp.zeros((128 - values.shape[0], rank), bf16)], axis=0)

    for b in range(n_px):
        center = coeff[pad + part * b:pad + part * (b + 1)]
        around, outer = [filled(halo[b:b + 3].reshape(n_side, rank))], [bias_side[...]]
        if b == 0:
            around, outer = around + [filled(rim[0])], outer + [bias_top[...]]
        if b == last:
            around, outer = around + [filled(rim[1])], outer + [bias_low[...]]
        sizes = jnp.concatenate([across(norms(values)) for values in around], axis=1)
        summed, mass = weigh(
            center, size_col[b, :, 2:3], size_col[b, :, 1:2],
            jnp.concatenate(around, axis=0), sizes, jnp.concatenate(outer, axis=1),
        )
        summed = center.astype(f32) + around_num[b] + summed
        avg_ref[b] = (summed / (1.0 + around_mass[b] + mass)).astype(bf16)

    for dz, dx in plane:
        remote(pieces.at[sx], pieces.at[sx], {"sx": at(dz, dx)}, plane_sem[dz, dx]).wait_send()
    for copy in sent:
        copy.wait_send()


def merge_tile(pieces, gath_ref, tile):
    gath_ref[tile] = pieces[tile].reshape(gath_ref.shape[1:])


def on_device(near, pix_total, patterns, basis, valid, strength):
    cells_x, cells_y, pixels = patterns.shape
    n_sx, n_sy, n_px = (lax.axis_size(name) for name in ("sx", "sy", "px"))
    depth = basis.shape[1]
    rank = depth * n_sx * n_sy
    part = cells_x * cells_y // n_px
    pad = RADIUS * cells_y
    bf16, f32 = jnp.bfloat16, jnp.float32
    n_copies = (n_sy - 1) + 2 * (n_sx // 2 - 1) + 1 + 2 * (n_px - 1) + 8
    n_wide = -(-(ROWS + 2 * RADIUS) * cells_y // 128) * 128
    vmem, hbm = pl.BlockSpec(memory_space=pltpu.VMEM), pl.BlockSpec(memory_space=pltpu.HBM)
    avg, gathered = pl.pallas_call(
        functools.partial(kernel, near, pix_total),
        out_shape=(
            jax.ShapeDtypeStruct((n_px, part, rank), bf16),
            jax.ShapeDtypeStruct((n_sx, depth * n_sy, pixels), bf16),
        ),
        in_specs=[hbm, hbm, hbm, hbm],
        out_specs=(vmem, vmem),
        scratch_shapes=[
            pltpu.VMEM((n_px * part, pixels), bf16),
            pltpu.VMEM((n_sx, n_sy, depth, pixels), bf16),
            pltpu.VMEM((part, rank), f32),
            pltpu.VMEM((n_px, part, rank), bf16),
            pltpu.VMEM((n_px, part, rank), bf16),
            pltpu.VMEM((n_wide + (n_px - 1) * part, rank), bf16),
            pltpu.VMEM((n_px, part, rank), bf16),
            pltpu.VMEM((2, pad, rank), bf16),
            pltpu.VMEM((n_px + 2, 2, ROWS * EDGE, rank), bf16),
            pltpu.VMEM((2, n_px, ROWS * EDGE, rank), bf16),
            pltpu.VMEM((2 * ROWS * EDGE, part), bf16),
            pltpu.VMEM((part, n_wide), f32),
            pltpu.VMEM((part, 128), f32),
            pltpu.VMEM((part, 128), f32),
            pltpu.VMEM((part, 128), f32),
            pltpu.VMEM((n_px, part, 128), f32),
            pltpu.VMEM((8, 128 + n_px * part + 512), f32),
            pltpu.VMEM((n_px, part, rank), f32),
            pltpu.VMEM((n_px, part, 1), f32),
            pltpu.VMEM(valid.shape, valid.dtype),
            pltpu.VMEM(strength.shape, strength.dtype),
            pltpu.SemaphoreType.DMA,
            pltpu.SemaphoreType.DMA,
            pltpu.SemaphoreType.DMA((2,)),
            pltpu.SemaphoreType.DMA((n_copies,)),
            pltpu.SemaphoreType.DMA((n_copies,)),
        ],
        compiler_params=pltpu.CompilerParams(collective_id=0, has_side_effects=True, vmem_limit_bytes=30 * 2**20),
    )(*[pltpu.with_memory_space_constraint(a, pltpu.HBM) for a in (patterns.reshape(cells_x * cells_y, pixels), basis.T, valid, strength)])
    rebuilt = jnp.dot(
        avg.reshape(cells_x * cells_y, rank), gathered.reshape(rank, pixels), preferred_element_type=f32
    )
    return rebuilt.astype(bf16).reshape(cells_x, cells_y, pixels)


def solution(mesh, near=NEAR, pix_total=9216):
    return jax.shard_map(
        functools.partial(on_device, near, pix_total),
        mesh=mesh,
        in_specs=(P("sx", "sy", "px"), P("px", ("sx", "sy")), P("sx", "sy"), P("sx", "sy")),
        out_specs=P("sx", "sy", "px"),
        check_vma=False,
    )
```

time: 59 us -> 51.3 us (0.87)
  Pallas kernels: 55.2 us -> 49 us
  matrix products: 3.55 us -> 2.19 us
    pallas_call x1, Pallas kernels: 55.2 us -> 49 us  [on_device(): pl.pallas_call(functools.partial(kernel, near, pix_total), out_shape=(jax...]
    dot_general x1, matrix products: 3.55 us -> 2.19 us  [on_device(): jnp.dot(avg.reshape(cells_x * cells_y, rank), gathered.reshape(rank, pixe...]
where the time goes in v2:
time: 51.3 us; the launch traced here: 51.2 us
  Pallas kernels  49 us (96%)
  matrix products  2.19 us (4%)
    pallas_call x1, Pallas kernels, on_device(): pl.pallas_call(functools.partial(kernel, near, pix_total), out_shape=(jax...  49 us
    dot_general x1, matrix products, on_device(): jnp.dot(avg.reshape(cells_x * cells_y, rank), gathered.reshape(rank, pixe...  2.19 us

profile of v2, /device:TPU:1, one launch (start us, length us, event | category | flops | bytes accessed | tf_op | source)
XLA Modules:
  0.0 51.2 jit_solution(5492973573818453023)
XLA Ops:
  0.0 49.0 %shard_map.46 = (bf16[4,128,256]{2,1,0:T(8,128)(2,1)S(1)}, bf16[16,16,2304]{2,1,0:T(8,128)(2,1)S(1)}) custom-call(bf16[512,2304]{1,0:T(8,128)(2,1)} %bitcast.9, bf16[2,2304]{1,0:T(2,128)(2,1)} %bitcast.10, s32[16,32]{1,0:T(8,128)} %valid_ref.1, f32[16,32]{1,0:T(8,128)} %strength_ref.1), custom_call_target="tpu_custom_call" | custom-call | tf_op jit(solution)/shard_map/pallas_call | solution.py:300
  49.0 2.2 %convolution_convert_fusion = bf16[512,2304]{1,0:T(8,128)(2,1)} fusion(bf16[512,256]{1,0:T(8,128)(2,1)S(1)} %bitcast.8, bf16[256,2304]{1,0:T(8,128)(2,1)S(1)} %bitcast.7), kind=kOutput, calls=%fused_computation | convolution fusion | flops 605159424 | bytes 3801088 | tf_op jit(solution)/shard_map/dot_general | solution.py:338

commit v3 on v2

--- a/solution.py
+++ b/solution.py
@@ -14,6 +14,7 @@
 FAR = 1e15
 OFF = 1e30
 EDGE = 4
+LAG = 3
 ROWS = 4
 NT = (((1,), (1,)), ((), ()))
 
@@ -57,7 +58,8 @@
     chip_x = (sx // n_core) % n_x
     chip_z = sx // (n_core * n_x)
     depth, pixels = pieces.shape[2], pieces.shape[3]
-    part, rank = own32.shape
+    part, half = own32.shape[1:]
+    rank = n_z * half
     cols = part // ROWS
     n_rows = n_px * ROWS
     pad = RADIUS * cols
@@ -115,8 +117,9 @@
     bias_side[...] = outside(side_row - my_row, side_col - my_col, lane < n_side)
     bias_top[...] = outside(lane // cols - RADIUS - my_row, lane % cols - my_col, lane < pad)
     bias_low[...] = outside(lane // cols + ROWS - my_row, lane % cols - my_col, lane < pad)
-    coeff[0:pad] = jnp.zeros((pad, rank), bf16)
-    coeff[pad + n_px * part:] = jnp.zeros((coeff.shape[0] - pad - n_px * part, rank), bf16)
+    n_tail = coeff.shape[1] - pad - n_px * part
+    coeff[:, 0:pad] = jnp.zeros((n_z, pad, half), bf16)
+    coeff[:, pad + n_px * part:] = jnp.zeros((n_z, n_tail, half), bf16)
     size_row[...] = jnp.full(size_row.shape, OFF, f32)
 
     load_basis.wait()
@@ -145,39 +148,52 @@
     along = {d: send(pieces.at[sx, sy], pieces.at[sx, sy], {"sy": (sy + d) % n_sy}) for d in order}
     plane_sem = {c: fresh() for c in plane}
 
-    def to_plane(y):
-        for dz, dx in plane:
+    def to_plane(y, targets):
+        for dz, dx in targets:
             remote(pieces.at[sx, y], pieces.at[sx, y], {"sx": at(dz, dx)}, plane_sem[dz, dx]).start()
 
-    to_plane(sy)
-    for d in reversed(order):
-        along[d].wait_recv()
-        to_plane((sy + n_sy - d) % n_sy)
-
-    passed = [(sx, send(pieces.at[sx], pieces.at[sx], {"sx": sibling}))]
-    merge_tile(pieces, gath_ref, sx)
-    for dz, dx in plane:
-        tile = at(-dz, -dx)
-        remote(pieces.at[tile], pieces.at[tile], {"sx": at(dz, dx)}, plane_sem[dz, dx]).wait_recv()
-        passed.append((tile, send(pieces.at[tile], pieces.at[tile], {"sx": sibling})))
-        merge_tile(pieces, gath_ref, tile)
-    for tile, copy in passed:
-        copy.wait_recv()
-        merge_tile(pieces, gath_ref, tile + 1 - 2 * core)
-    load.wait()
-
-    whole = gath_ref[...].reshape(rank, pixels)
-
-    def project(which):
-        block = pat[pl.ds(pl.multiple_of(which * part, part), part), :]
-        return lax.dot_general(block, whole, NT, preferred_element_type=f32)
-
+    soon = [c for c in plane if c[0] == 0 or c[1] == 0]
+    later = [c for c in plane if c not in soon]
+    held = []
+    for d in [0] + order[::-1]:
+        if d:
+            along[d].wait_recv()
+        y = (sy + n_sy - d) % n_sy
+        to_plane(y, soon)
+        held.append(y)
+        if len(held) > LAG:
+            to_plane(held.pop(0), later)
+    for y in held:
+        to_plane(y, later)
+
+    tiles = n_sx // n_z
+    far_first = sorted(range(1, n_px), key=lambda d: -min(d, n_px - d))
     reduce = []
-    far_first = sorted(range(1, n_px), key=lambda d: -min(d, n_px - d))
-    for d in far_first:
-        part16[d] = project((px + d) % n_px).astype(bf16)
-        reduce.append(send(part16.at[d], arrived.at[d], {"px": (px + d) % n_px}))
-    own32[...] = project(px)
+    for step in range(n_z):
+        passed = []
+        for dz, dx in [(step, 0)] + [c for c in plane if c[0] == step and c[1]]:
+            tile = at(-dz, -dx)
+            if (dz, dx) != (0, 0):
+                remote(pieces.at[tile], pieces.at[tile], {"sx": at(dz, dx)}, plane_sem[dz, dx]).wait_recv()
+            passed.append((tile, send(pieces.at[tile], pieces.at[tile], {"sx": sibling})))
+            merge_tile(pieces, gath_ref, tile)
+        for tile, copy in passed:
+            copy.wait_recv()
+            merge_tile(pieces, gath_ref, tile + 1 - 2 * core)
+        if step == 0:
+            load.wait()
+        which = (chip_z + n_z - step) % n_z
+        basis_half = gath_ref[pl.ds(which * tiles, tiles)].reshape(half, pixels)
+
+        def project(to):
+            block = pat[pl.ds(pl.multiple_of(to * part, part), part), :]
+            return lax.dot_general(block, basis_half, NT, preferred_element_type=f32)
+
+        for d in far_first:
+            part16[step, d] = project((px + d) % n_px).astype(bf16)
+            reduce.append(send(part16.at[step, d], arrived.at[step, d], {"px": (px + d) % n_px}))
+        own32[step] = project(px)
+
     for copy in load_maps:
         copy.wait()
     valid = jnp.transpose(valid_v[...].astype(f32))
@@ -186,20 +202,27 @@
         for r in range(ROWS):
             size_col[b, cols * r:cols * (r + 1), 0:1] = valid[:, ROWS * b + r:ROWS * b + r + 1]
             size_col[b, cols * r:cols * (r + 1), 1:2] = factor[:, ROWS * b + r:ROWS * b + r + 1]
-    for copy in reduce:
-        copy.wait_recv()
-    total = own32[...]
-    for d in range(1, n_px):
-        total = total + arrived[d].astype(f32)
-
-    def slot(which):
-        return coeff.at[pl.ds(pl.multiple_of(pad + which * part, ROWS * EDGE), part)]
-
-    slot(px)[...] = total.astype(bf16)
-    spread = [(d, send(slot(px), slot(px), {"px": (px + d) % n_px})) for d in far_first]
+
+    def rows_of(which):
+        return pl.ds(pl.multiple_of(pad + which * part, ROWS * EDGE), part)
+
+    spread = []
+    for step in range(n_z):
+        which = (chip_z + n_z - step) % n_z
+        for copy in reduce[step * len(far_first):(step + 1) * len(far_first)]:
+            copy.wait_recv()
+        total = own32[step]
+        for d in range(1, n_px):
+            total = total + arrived[step, d].astype(f32)
+        mine = coeff.at[which, rows_of(px)]
+        mine[...] = total.astype(bf16)
+        spread += [(d, send(mine, mine, {"px": (px + d) % n_px})) for d in far_first]
+
+    def sums(start, count):
+        return jnp.concatenate([coeff[z, start:start + count] for z in range(n_z)], axis=1)
 
     def look(which):
-        values = slot(which)[...]
+        values = jnp.concatenate([coeff[z, rows_of(which)] for z in range(n_z)], axis=1)
         on = size_col[which, :, 0:1] > 0.5
         size = norms(values)
         size_col[which, :, 2:3] = size
@@ -210,19 +233,21 @@
         pack[1, which] = edges[ROWS * EDGE:]
 
     look(px)
-    for d, copy in reversed(spread):
-        copy.wait_recv()
+    for d in far_first[::-1]:
+        for e, copy in spread:
+            if e == d:
+                copy.wait_recv()
         look((px + n_px - d) % n_px)
     last = n_px - 1
     swap = [
-        send(seen.at[0, pl.ds(0, pad)], rim.at[1], {"sx": down}),
-        send(seen.at[last, pl.ds(part - pad, pad)], rim.at[0], {"sx": up}),
         send(pack.at[0, 0], halo.at[n_px + 1, 0], {"sx": down, "sy": left}),
         send(pack.at[0, last], halo.at[0, 0], {"sx": up, "sy": left}),
         send(pack.at[1, 0], halo.at[n_px + 1, 1], {"sx": down, "sy": right}),
         send(pack.at[1, last], halo.at[0, 1], {"sx": up, "sy": right}),
         send(pack.at[0], halo.at[pl.ds(1, n_px), 0], {"sy": left}),
         send(pack.at[1], halo.at[pl.ds(1, n_px), 1], {"sy": right}),
+        send(seen.at[0, pl.ds(0, pad)], rim.at[1], {"sx": down}),
+        send(seen.at[last, pl.ds(part - pad, pad)], rim.at[0], {"sx": up}),
     ]
 
     for b in range(n_px):
@@ -230,11 +255,11 @@
         size_row[0:1, 128 * b + 128:128 * b + 128 + part] = across(column)
     n_wide = bias.shape[1]
     for b in range(n_px):
-        center = coeff[pad + part * b:pad + part * (b + 1)]
+        center = sums(pad + part * b, part)
         lanes = 128 - pad + part * b
-        sizes = jnp.concatenate([size_row[0:1, lanes:lanes + n_wide]], axis=1)
+        sizes = size_row[0:1, lanes:lanes + n_wide]
         around_num[b], around_mass[b] = weigh(
-            center, size_col[b, :, 2:3], size_col[b, :, 1:2], coeff[part * b:part * b + n_wide], sizes, bias[...]
+            center, size_col[b, :, 2:3], size_col[b, :, 1:2], sums(part * b, n_wide), sizes, bias[...]
         )
 
     for copy in swap:
@@ -262,7 +287,7 @@
         return jnp.concatenate([values, jnp.zeros((128 - values.shape[0], rank), bf16)], axis=0)
 
     for b in range(n_px):
-        center = coeff[pad + part * b:pad + part * (b + 1)]
+        center = sums(pad + part * b, part)
         around, outer = [filled(halo[b:b + 3].reshape(n_side, rank))], [bias_side[...]]
         if b == 0:
             around, outer = around + [filled(rim[0])], outer + [bias_top[...]]
@@ -286,6 +311,19 @@
     gath_ref[tile] = pieces[tile].reshape(gath_ref.shape[1:])
 
 
+def rebuild(avg_ref, basis_ref, out_ref, made, sem):
+    n_parts, _, n_lanes = made.shape
+    copies = []
+    for i in range(n_parts):
+        lanes = pl.ds(i * n_lanes, n_lanes)
+        product = jnp.dot(avg_ref[...], basis_ref[:, lanes], preferred_element_type=jnp.float32)
+        made[i] = product.astype(made.dtype)
+        copies.append(pltpu.make_async_copy(made.at[i], out_ref.at[:, lanes], sem.at[i]))
+        copies[-1].start()
+    for copy in copies:
+        copy.wait()
+
+
 def on_device(near, pix_total, patterns, basis, valid, strength):
     cells_x, cells_y, pixels = patterns.shape
     n_sx, n_sy, n_px = (lax.axis_size(name) for name in ("sx", "sy", "px"))
@@ -294,7 +332,9 @@
     part = cells_x * cells_y // n_px
     pad = RADIUS * cells_y
     bf16, f32 = jnp.bfloat16, jnp.float32
-    n_copies = (n_sy - 1) + 2 * (n_sx // 2 - 1) + 1 + 2 * (n_px - 1) + 8
+    n_z = near[0]
+    half = rank // n_z
+    n_copies = (n_sy - 1) + 2 * (n_sx // 2 - 1) + 1 + 2 * n_z * (n_px - 1) + 8
     n_wide = -(-(ROWS + 2 * RADIUS) * cells_y // 128) * 128
     vmem, hbm = pl.BlockSpec(memory_space=pltpu.VMEM), pl.BlockSpec(memory_space=pltpu.HBM)
     avg, gathered = pl.pallas_call(
@@ -308,10 +348,10 @@
         scratch_shapes=[
             pltpu.VMEM((n_px * part, pixels), bf16),
             pltpu.VMEM((n_sx, n_sy, depth, pixels), bf16),
-            pltpu.VMEM((part, rank), f32),
-            pltpu.VMEM((n_px, part, rank), bf16),
-            pltpu.VMEM((n_px, part, rank), bf16),
-            pltpu.VMEM((n_wide + (n_px - 1) * part, rank), bf16),
+            pltpu.VMEM((n_z, part, half), f32),
+            pltpu.VMEM((n_z, n_px, part, half), bf16),
+            pltpu.VMEM((n_z, n_px, part, half), bf16),
+            pltpu.VMEM((n_z, n_wide + (n_px - 1) * part, half), bf16),
             pltpu.VMEM((n_px, part, rank), bf16),
             pltpu.VMEM((2, pad, rank), bf16),
             pltpu.VMEM((n_px + 2, 2, ROWS * EDGE, rank), bf16),
@@ -335,10 +375,17 @@
         ],
         compiler_params=pltpu.CompilerParams(collective_id=0, has_side_effects=True, vmem_limit_bytes=30 * 2**20),
     )(*[pltpu.with_memory_space_constraint(a, pltpu.HBM) for a in (patterns.reshape(cells_x * cells_y, pixels), basis.T, valid, strength)])
-    rebuilt = jnp.dot(
-        avg.reshape(cells_x * cells_y, rank), gathered.reshape(rank, pixels), preferred_element_type=f32
-    )
-    return rebuilt.astype(bf16).reshape(cells_x, cells_y, pixels)
+    n_cells, n_lanes = cells_x * cells_y, 256
+    n_parts = pixels // n_lanes
+    rebuilt = pl.pallas_call(
+        rebuild,
+        out_shape=jax.ShapeDtypeStruct((n_cells, pixels), bf16),
+        in_specs=[vmem, vmem],
+        out_specs=pl.BlockSpec(memory_space=pl.ANY),
+        scratch_shapes=[pltpu.VMEM((n_parts, n_cells, n_lanes), bf16), pltpu.SemaphoreType.DMA((n_parts,))],
+        compiler_params=pltpu.CompilerParams(vmem_limit_bytes=30 * 2**20),
+    )(avg.reshape(n_cells, rank), gathered.reshape(rank, pixels))
+    return rebuilt.reshape(cells_x, cells_y, pixels)
 
 
 def solution(mesh, near=NEAR, pix_total=9216):

time: 51.3 us -> 49.1 us (0.957)
  matrix products: 2.19 us -> 0 us
    dot_general x1 -> x0, matrix products: 2.19 us -> none  [on_device(): jnp.dot(avg.reshape(cells_x * cells_y, rank), gathered.reshape(rank, pixe...]
    pallas_call x1, Pallas kernels: 49 us -> 47.2 us  [on_device(): pl.pallas_call(functools.partial(kernel, near, pix_total), out_shape=(jax...]
    pallas_call x0 -> x1, Pallas kernels: none -> 1.76 us  [on_device(): pl.pallas_call(rebuild, out_shape=jax.ShapeDtypeStruct((n_cells, pixels),...]
where the time goes in v3:
time: 49.1 us; the launch traced here: 49 us
  Pallas kernels  48.9 us (100%)
    pallas_call x1, Pallas kernels, on_device(): pl.pallas_call(functools.partial(kernel, near, pix_total), out_shape=(jax...  47.2 us
    pallas_call x1, Pallas kernels, on_device(): pl.pallas_call(rebuild, out_shape=jax.ShapeDtypeStruct((n_cells, pixels),...  1.76 us

profile of v3, /device:TPU:1, one launch (start us, length us, event | category | flops | bytes accessed | tf_op | source)
XLA Modules:
  0.0 49.0 jit_solution(5520539369346814003)
XLA Ops:
  0.0 47.2 %shard_map.46 = (bf16[4,128,256]{2,1,0:T(8,128)(2,1)S(1)}, bf16[16,16,2304]{2,1,0:T(8,128)(2,1)S(1)}) custom-call(bf16[512,2304]{1,0:T(8,128)(2,1)} %bitcast.7, bf16[2,2304]{1,0:T(2,128)(2,1)} %bitcast.8, s32[16,32]{1,0:T(8,128)} %valid_ref.1, f32[16,32]{1,0:T(8,128)} %strength_ref.1), custom_call_target="tpu_custom_call" | custom-call | tf_op jit(solution)/shard_map/pallas_call | solution.py:340
  47.2 1.8 %shard_map.47 = bf16[512,2304]{1,0:T(8,128)(2,1)} custom-call(bf16[512,256]{1,0:T(8,128)(2,1)S(1)} %bitcast.6, bf16[256,2304]{1,0:T(8,128)(2,1)S(1)} %bitcast.5), custom_call_target="tpu_custom_call" | custom-call | tf_op jit(solution)/shard_map/pallas_call | solution.py:380

commit v4 on v3

--- a/solution.py
+++ b/solution.py
@@ -152,8 +152,8 @@
         for dz, dx in targets:
             remote(pieces.at[sx, y], pieces.at[sx, y], {"sx": at(dz, dx)}, plane_sem[dz, dx]).start()
 
-    soon = [c for c in plane if c[0] == 0 or c[1] == 0]
-    later = [c for c in plane if c not in soon]
+    soon = [c for c in plane[::-1] if c[0] == 0 or c[1] == 0]
+    later = [c for c in plane[::-1] if c not in soon]
     held = []
     for d in [0] + order[::-1]:
         if d:
@@ -176,6 +176,7 @@
             if (dz, dx) != (0, 0):
                 remote(pieces.at[tile], pieces.at[tile], {"sx": at(dz, dx)}, plane_sem[dz, dx]).wait_recv()
             passed.append((tile, send(pieces.at[tile], pieces.at[tile], {"sx": sibling})))
+        for tile, _ in passed:
             merge_tile(pieces, gath_ref, tile)
         for tile, copy in passed:
             copy.wait_recv()
@@ -224,14 +225,15 @@
     def look(which):
         values = jnp.concatenate([coeff[z, rows_of(which)] for z in range(n_z)], axis=1)
         on = size_col[which, :, 0:1] > 0.5
-        size = norms(values)
-        size_col[which, :, 2:3] = size
         shown = jnp.where(on, values.astype(f32), FAR).astype(bf16)
         seen[which] = shown
         edges = jnp.dot(pick[...], shown, preferred_element_type=f32).astype(bf16)
         pack[0, which] = edges[:ROWS * EDGE]
         pack[1, which] = edges[ROWS * EDGE:]
-
+        swap.append(send(pack.at[0, which], halo.at[which + 1, 0], {"sy": left}))
+        swap.append(send(pack.at[1, which], halo.at[which + 1, 1], {"sy": right}))
+
+    swap = []
     look(px)
     for d in far_first[::-1]:
         for e, copy in spread:
@@ -239,18 +241,17 @@
                 copy.wait_recv()
         look((px + n_px - d) % n_px)
     last = n_px - 1
-    swap = [
+    swap += [
         send(pack.at[0, 0], halo.at[n_px + 1, 0], {"sx": down, "sy": left}),
         send(pack.at[0, last], halo.at[0, 0], {"sx": up, "sy": left}),
         send(pack.at[1, 0], halo.at[n_px + 1, 1], {"sx": down, "sy": right}),
         send(pack.at[1, last], halo.at[0, 1], {"sx": up, "sy": right}),
-        send(pack.at[0], halo.at[pl.ds(1, n_px), 0], {"sy": left}),
-        send(pack.at[1], halo.at[pl.ds(1, n_px), 1], {"sy": right}),
         send(seen.at[0, pl.ds(0, pad)], rim.at[1], {"sx": down}),
         send(seen.at[last, pl.ds(part - pad, pad)], rim.at[0], {"sx": up}),
     ]
 
     for b in range(n_px):
+        size_col[b, :, 2:3] = norms(sums(pad + part * b, part))
         column = jnp.where(size_col[b, :, 0:1] > 0.5, size_col[b, :, 2:3], OFF)
         size_row[0:1, 128 * b + 128:128 * b + 128 + part] = across(column)
     n_wide = bias.shape[1]
@@ -334,7 +335,7 @@
     bf16, f32 = jnp.bfloat16, jnp.float32
     n_z = near[0]
     half = rank // n_z
-    n_copies = (n_sy - 1) + 2 * (n_sx // 2 - 1) + 1 + 2 * n_z * (n_px - 1) + 8
+    n_copies = (n_sy - 1) + 2 * (n_sx // 2 - 1) + 1 + 2 * n_z * (n_px - 1) + 6 + 2 * n_px
     n_wide = -(-(ROWS + 2 * RADIUS) * cells_y // 128) * 128
     vmem, hbm = pl.BlockSpec(memory_space=pltpu.VMEM), pl.BlockSpec(memory_space=pltpu.HBM)
     avg, gathered = pl.pallas_call(

time: 49.1 us -> 49 us (level)
  no operation moved by 1% of the time
where the time goes in v4:
time: 49 us; the launch traced here: 48.9 us
  Pallas kernels  48.9 us (100%)
    pallas_call x1, Pallas kernels, on_device(): pl.pallas_call(functools.partial(kernel, near, pix_total), out_shape=(jax...  47.1 us
    pallas_call x1, Pallas kernels, on_device(): pl.pallas_call(rebuild, out_shape=jax.ShapeDtypeStruct((n_cells, pixels),...  1.76 us

profile of v4, /device:TPU:1, one launch (start us, length us, event | category | flops | bytes accessed | tf_op | source)
XLA Modules:
  0.0 48.9 jit_solution(10344121722484495025)
XLA Ops:
  0.0 47.1 %shard_map.46 = (bf16[4,128,256]{2,1,0:T(8,128)(2,1)S(1)}, bf16[16,16,2304]{2,1,0:T(8,128)(2,1)S(1)}) custom-call(bf16[512,2304]{1,0:T(8,128)(2,1)} %bitcast.7, bf16[2,2304]{1,0:T(2,128)(2,1)} %bitcast.8, s32[16,32]{1,0:T(8,128)} %valid_ref.1, f32[16,32]{1,0:T(8,128)} %strength_ref.1), custom_call_target="tpu_custom_call" | custom-call | tf_op jit(solution)/shard_map/pallas_call | solution.py:341
  47.1 1.8 %shard_map.47 = bf16[512,2304]{1,0:T(8,128)(2,1)} custom-call(bf16[512,256]{1,0:T(8,128)(2,1)S(1)} %bitcast.6, bf16[256,2304]{1,0:T(8,128)(2,1)S(1)} %bitcast.5), custom_call_target="tpu_custom_call" | custom-call | tf_op jit(solution)/shard_map/pallas_call | solution.py:381
